TPU v7x, 256 devices: a whole 4x4x8 slice. The times are simulated.
256 devices in a mesh: seq: 16 (over z, x_lo), img: 8 (over y, x_hi), fsdp: 2 (over core).
Axes of the slice: x: 4 (x_hi: 2, x_lo: 2; x = x_hi * 2 + x_lo), y: 4, z: 8, core: 2. Of those that a mesh axis runs over, the one named last changes fastest.
Arguments:
- vision_feats: bfloat16 [8, 2304, 1024], P('img', ('seq', 'fsdp')), may hold values from -6 to 6
- ln_gain: float32 [1024], replicated, may hold values from 0.5 to 1.5
- ln_bias: float32 [1024], replicated, may hold values from -3 to 3
- w_in: bfloat16 [1024, 4096], P('fsdp', 'seq'), may hold values from -0.1875 to 0.1875
- b_in: float32 [4096], P('seq'), may hold values from -3 to 3
- w_out: bfloat16 [4096, 4096], P('seq', 'fsdp'), may hold values from -0.09375 to 0.09375
- lm_grad: bfloat16 [8, 4096, 4096], P('img', 'seq', 'fsdp'), may hold values from -0.079589844 to 0.079589844
- image_counts: int32 [8, 2], P('img'), may hold values from 1 to 3, as said below
- token_pos: int32 [8, 2304], P('img'), may hold values from 0 to 2047, as said below
Outputs:
- w_in_grad: float32 [1024, 4096], P(('img', 'fsdp'), 'seq')
- b_in_grad: float32 [4096], replicated
- w_out_grad: float32 [4096, 4096], P(('seq', 'img'), 'fsdp')
- b_out_grad: float32 [4096], replicated
- ln_gain_grad: float32 [1024], replicated
- ln_bias_grad: float32 [1024], replicated
Inputs may be any that keep to these rules, and one draw needn't show every extreme that they name: `image_counts`: in each group the 2 samples hold 4 images together, each sample one or more. `token_pos`: each image's 576 tokens take consecutive positions of its sample's sequence in order; a sample's images come in order without intersection, and images are numbered sample by sample as image_counts gives.
All inputs are finite; a program needn't handle non-finite values.
Results may differ from a plain program's by a relative error of at most 0.0047.
Values may be sent and summed in bfloat16 or wider, within the bound.
No kernel may reach another device: no remote copies, remote signals or barrier semaphores. Data moves between devices by JAX's collectives and lax.ppermute only.
A program may use at most 128 MiB of HBM per device.

v0:
```python
import jax
import jax.numpy as jnp
from jax import lax
from jax.sharding import Mesh
from jax.sharding import PartitionSpec as P

PATCH = 576
LEN = 2048
SEQ = ("seq_0", "seq_1")
IMG = ("img_0", "img_1")
SEQ_FSDP = ("seq_0", "seq_1", "fsdp")
SEQ_IMG_FSDP = ("seq_0", "seq_1", "img_0", "img_1", "fsdp")
IMG_FSDP = ("img_0", "img_1", "fsdp")
SEQ_IMG = ("seq_0", "seq_1", "img_0", "img_1")


def copy_for_each(array, axis):
    copies = jnp.broadcast_to(array, (lax.axis_size(axis), *array.shape))
    return lax.all_to_all(copies, axis, split_axis=0, concat_axis=0, tiled=True)


def in_order(pieces, dim):
    shape = list(pieces.shape[1:])
    shape[dim] *= pieces.shape[0]
    return jnp.moveaxis(pieces, 0, dim).reshape(shape)


def gather_directly(array, axis, dim):
    pieces = copy_for_each(array, axis)
    return in_order(pieces, dim)


def whole_of(array, axes, dim):
    if not axes:
        return array
    nearer = lax.all_gather(array, axes[-1], axis=dim, tiled=True)
    return whole_of(nearer, axes[:-1], dim)


def taken_together(array, axis):
    return copy_for_each(array, axis).sum(axis=0)


def in_blocks(array, dim, devices):
    shape = array.shape
    pieces = array.reshape(*shape[:dim], devices, shape[dim] // devices, *shape[dim + 1 :])
    return jnp.moveaxis(pieces, dim, 0)


def one_scatter(arrays, axis, dims):
    devices = lax.axis_size(axis)
    pieces = [in_blocks(a, dim, devices) for a, dim in zip(arrays, dims)]
    lines = jnp.concatenate([b.reshape(devices, -1) for b in pieces], axis=1)
    width = max(16, -(-lines.shape[1] // 1024) * 8)
    lines = jnp.pad(lines, ((0, 0), (0, width * 128 - lines.shape[1]))).reshape(-1, 128)
    vector, at, gathered = (lax.psum_scatter(lines, axis, tiled=True).reshape(-1), 0, [])
    for b in pieces:
        part = b[0]
        gathered.append(vector[at : at + part.size].reshape(part.shape))
        at += part.size
    return tuple(gathered)


def one_axis_at_a_time(array, axes):
    for axis in axes:
        array = lax.psum(array, axis)
    return array


def gelu_parts(preact):
    cumul = 0.5 * (1.0 + lax.erf(preact * 0.7071067811865476))
    density = jnp.exp(-0.5 * preact * preact) * 0.3989422804014327
    return (preact * cumul, cumul + preact * density)


def contract(left, right, left_dim, right_dim):
    return lax.dot_general(
        left, right, (((left_dim,), (right_dim,)), ((), ())), preferred_element_type=jnp.float32
    )


def own_columns(matrix, img_count, fsdp_count, fsdp_index):
    rows = matrix.shape[0]
    block = matrix.shape[1] // (img_count * fsdp_count)
    shaped = matrix.reshape(rows, img_count, fsdp_count, block)
    taken = lax.dynamic_index_in_dim(shaped, fsdp_index, axis=2, keepdims=False)
    return taken.reshape(rows, img_count * block)


def place_columns(vector, img_count, fsdp_count, fsdp_index):
    block = vector.shape[0] // img_count
    holder = jnp.zeros((img_count, fsdp_count, block), jnp.float32)
    holder = lax.dynamic_update_slice(
        holder, vector.reshape(img_count, 1, block), (0, fsdp_index, 0)
    )
    return holder.reshape(img_count * fsdp_count * block)


def per_device(vision_feats, ln_gain, ln_bias, w_in, b_in, w_out, lm_grad, image_counts, token_pos):
    seq_count = lax.axis_size(SEQ)
    seq_index = lax.axis_index(SEQ)
    img_count = lax.axis_size(IMG)
    fsdp_count = lax.axis_size("fsdp")
    fsdp_index = lax.axis_index("fsdp")
    lm_block = lm_grad[0]
    block_rows = lm_block.shape[0]
    half_width = lm_block.shape[1]
    position_count = block_rows * seq_count
    counts = image_counts[0]
    positions = token_pos[0]
    row_count = positions.shape[0]
    image_index = jnp.arange(row_count, dtype=jnp.int32) // PATCH
    bounds = jnp.cumsum(counts)
    sample = jnp.sum((image_index[:, None] >= bounds[None, :]).astype(jnp.int32), axis=1)
    abs_pos = sample * LEN + positions
    marker = jnp.zeros((position_count,), jnp.float32).at[abs_pos].set(1.0)
    own_mask = lax.dynamic_slice_in_dim(marker, seq_index * block_rows, block_rows).astype(
        jnp.bfloat16
    )
    out_bias_half = jnp.dot(own_mask[None, :], lm_block, preferred_element_type=jnp.float32)[0]
    out_bias_full = lax.dynamic_update_slice_in_dim(
        jnp.zeros((half_width * fsdp_count,), jnp.float32),
        out_bias_half,
        fsdp_index * half_width,
        0,
    )
    w_in_full = gather_directly(w_in, "fsdp", 0)
    gathered = lax.all_gather(vision_feats[0], SEQ_FSDP, axis=0, tiled=True)
    values = gathered.astype(jnp.float32)
    row_mean = jnp.mean(values, axis=1, keepdims=True)
    centred = values - row_mean
    row_var = jnp.mean(centred * centred, axis=1, keepdims=True)
    normed = centred * lax.rsqrt(row_var + 1e-05)
    normed_in = (normed * ln_gain + ln_bias).astype(jnp.bfloat16)
    preact = jnp.dot(normed_in, w_in_full, preferred_element_type=jnp.float32) + b_in
    activ, slope = gelu_parts(preact)
    hidden = activ.astype(jnp.bfloat16)
    hidden_width = hidden.shape[1]
    whole_grad = whole_of(lm_block, SEQ, 0)
    picked = whole_grad[abs_pos]
    hidden_part = contract(picked, w_out, 1, 1)
    w_out_part = contract(hidden, picked, 0, 0)
    hidden_grad = taken_together(hidden_part, "fsdp")
    preact_grad = (hidden_grad * slope).astype(jnp.bfloat16)
    own_normed_in = own_columns(normed_in, img_count, fsdp_count, fsdp_index)
    own_normed = own_columns(normed, img_count, fsdp_count, fsdp_index)
    own_w_in = own_columns(w_in_full.T, img_count, fsdp_count, fsdp_index)
    w_in_part = contract(own_normed_in, preact_grad, 0, 0)
    half_rows = row_count // fsdp_count
    own_rows = lax.dynamic_slice_in_dim(preact_grad, fsdp_index * half_rows, half_rows, 0)
    b_in_part = jnp.sum(own_rows, axis=0, dtype=jnp.float32)
    normed_grad = contract(preact_grad, own_w_in, 1, 0)
    gain_part = place_columns(
        jnp.sum(normed_grad * own_normed, axis=0), img_count, fsdp_count, fsdp_index
    )
    bias_part = place_columns(jnp.sum(normed_grad, axis=0), img_count, fsdp_count, fsdp_index)
    w_in_grad, w_out_grad = one_scatter((w_in_part, w_out_part), IMG, (0, 0))
    hidden_full = lax.dynamic_update_slice_in_dim(
        jnp.zeros((hidden_width * seq_count,), jnp.float32), b_in_part, seq_index * hidden_width, 0
    )
    gain_grad, bias_grad, b_in_grad, b_out_grad = (
        one_axis_at_a_time(gain_part, SEQ_IMG_FSDP),
        one_axis_at_a_time(bias_part, SEQ_IMG_FSDP),
        one_axis_at_a_time(hidden_full, SEQ_IMG_FSDP),
        one_axis_at_a_time(out_bias_full, SEQ_IMG_FSDP),
    )
    return (w_in_grad, b_in_grad, w_out_grad, b_out_grad, gain_grad, bias_grad)


def solution(mesh):
    finer = Mesh(
        mesh.devices.reshape(8, 2, 4, 2, mesh.shape["fsdp"]),
        ("seq_0", "seq_1", "img_0", "img_1", "fsdp"),
    )
    placed = (
        P(IMG, SEQ_FSDP, None),
        P(),
        P(),
        P("fsdp", SEQ),
        P(SEQ),
        P(SEQ, "fsdp"),
        P(IMG, SEQ, "fsdp"),
        P(IMG, None),
        P(IMG, None),
    )
    return jax.shard_map(
        per_device,
        mesh=finer,
        in_specs=placed,
        out_specs=(P(IMG_FSDP, SEQ), P(), P(SEQ_IMG, "fsdp"), P(), P(), P()),
        check_vma=False,
    )
```

profile of v0, /device:TPU:1, one launch (start us, length us, event | category | flops | bytes accessed | tf_op | source)
XLA Modules:
  0.0 471.8 jit_solution(9273449355537463096)
XLA Ops:
  7.3 0.7 all-gather.9.cloned.1.call-update
  8.0 0.7 all-gather.7.cloned.1.call-update
  8.7 42.9 %all-gather.9.cloned.1.call-done = bf16[1,512,2048]{2,1,0:T(8,128)(2,1)} async-done(((bf16[1,256,2048]{2,1,0:T(8,128)(2,1)}), bf16[1,512,2048]{2,1,0:T(8,128)(2,1)}) %all-gather.9.cloned.1.call-update) | async-done | bytes 2097168 | tf_op jit(solution)/shard_map/all_gather | solution.py:36
  51.7 0.2 reduce-window.8
  51.9 0.1 fusion.13
  52.0 70.0 %all-gather.7.cloned.1.call-done = bf16[1,2304,1024]{2,1,0:T(8,128)(2,1)} async-done(((bf16[1,72,1024]{2,1,0:T(8,128)(2,1)}), bf16[1,2304,1024]{2,1,0:T(8,128)(2,1)}) %all-gather.7.cloned.1.call-update) | async-done | bytes 4718608 | tf_op jit(solution)/shard_map/all_gather | solution.py:128
  122.1 6.8 %copy.20 = bf16[1,2304,1024]{1,2,0:T(8,128)(2,1)} copy(bf16[1,2304,1024]{2,1,0:T(8,128)(2,1)} %all-gather.7.cloned.1.call-done) | data formatting | bytes 9437184 | tf_op jit(solution)/shard_map/all_gather | solution.py:128
  128.9 3.2 convert_reduce_fusion
  132.1 0.6 copy-done.2
  132.6 1.3 fusion.3
  133.9 4.8 %fusion.1 = (f32[2304,1024]{0,1:T(8,128)}, bf16[2304,1024]{0,1:T(8,128)(2,1)S(1)}) fusion(bf16[1,2304,1024]{1,2,0:T(8,128)(2,1)S(1)} %copy-done.2, f32[2304]{0:T(1024)S(1)} %add_rsqrt_fusion, f32[2304]{0:T(1024)S(1)} %broadcast_multiply_fusion.1, f32[1024]{0:T(1024)S(1)} %copy-done.10, f32[1024]{0:T(1024)S(1)} %copy-done.11), kind=kLoop, calls=%fused_computation.5 | loop fusion | flops 14155776 | bytes 18900992 | tf_op jit(solution)/shard_map/mul | solution.py:133
  138.7 2.1 copy-done.3
  140.9 1.6 constant_dynamic-slice_fusion.2
  142.5 153.5 %all-gather.11.cloned.1.call-done = bf16[1,4096,2048]{2,1,0:T(8,128)(2,1)} async-done(((bf16[1,512,2048]{2,1,0:T(8,128)(2,1)}), bf16[1,4096,2048]{2,1,0:T(8,128)(2,1)}) %all-gather.11.cloned.1.call-update) | async-done | bytes 16777232 | tf_op jit(solution)/shard_map/all_gather | solution.py:36
  296.0 26.2 %gather_fusion = bf16[2304,2048]{1,0:T(8,128)(2,1)} fusion(bf16[4096,2048]{1,0:T(8,128)(2,1)} %bitcast.43, s32[3072]{0:T(1024)S(1)} %pad_clamp_fusion), kind=kCustom, calls=%fused_computation | custom fusion | bytes 18883584 | tf_op jit(solution)/shard_map/gather | solution.py:140
  322.2 5.2 %fusion.21 = f32[2304,256]{1,0:T(8,128)S(1)} fusion(bf16[2304,2048]{1,0:T(8,128)(2,1)} %gather_fusion, bf16[256,2048]{1,0:T(8,128)(2,1)S(1)} %copy-done), kind=kOutput, calls=%fused_computation.48 | convolution fusion | flops 2415919104 | bytes 12845056 | tf_op jit(solution)/shard_map/dot_general | solution.py:77
  327.5 0.3 broadcast_in_dim.6
  327.8 9.2 %all_to_all.10 = f32[2,2304,256]{2,1,0:T(8,128)} all-to-all(f32[2,2304,256]{2,1,0:T(8,128)S(1)} %broadcast_in_dim.6), channel_id=1, replica_groups=mesh['seq_0'=8,'seq_1'=2,'img_0'=4,'img_1'=2,'fsdp'=2] {'fsdp'}, dimensions={0} | all-to-all | bytes 9437184 | tf_op jit(solution)/shard_map/all_to_all | solution.py:19
  337.0 0.8 broadcast_in_dim.7
  337.9 3.8 all-to-all-start.1
  341.7 4.5 reduce_sum.66
  346.2 6.7 %fusion.9 = (bf16[2304,256]{1,0:T(8,128)(2,1)}, f32[2304,256]{1,0:T(8,128)S(1)}) fusion(f32[2304,256]{1,0:T(8,128)} %reduce_sum.66, f32[256]{0:T(256)S(1)} %copy-done.12, bf16[2304,1024]{0,1:T(8,128)(2,1)} %copy-done.3, bf16[1024,256]{1,0:T(8,128)(2,1)S(1)} %bitcast.50), kind=kOutput, calls=%fused_computation.18 | convolution fusion | flops 1214447616 | bytes 11142144 | tf_op jit(solution)/shard_map/dot_general | solution.py:135
  352.9 4.0 fusion.10
  356.9 2.0 reshape_reshape.7
  358.9 2.8 fusion.22
  361.7 0.1 reshape_reshape.6
  361.8 1.7 pad_maximum_fusion
  363.5 3.6 reshape.151
  367.1 9.0 %scatter_custom_fusion = f32[4096]{0:T(1024)S(1)} fusion(s32[2304]{0:T(1024)S(1)} %fusion.17, f32[2304]{0:T(1024)S(1)} %broadcast.81, f32[]{:T(128)} %constant.22.clone.1), kind=kCustom, calls=%fused_computation.39 | custom fusion | bytes 16388 | tf_op jit(solution)/shard_map/scatter | solution.py:116
  376.1 0.1 dynamic_slice.28
  376.2 0.2 fusion.11
  376.5 0.2 dynamic_update_slice.13
  376.7 5.0 %constant_dynamic-slice_fusion = f32[2304,8,1,64]{0,3,2,1:T(8,128)} fusion(f32[2304,8,2,64]{0,3,2,1:T(8,128)} %bitcast.46, s32[]{:T(128)S(6)} %select_n.40), kind=kLoop, calls=%fused_computation.44 | loop fusion | bytes 9437188 | tf_op jit(solution)/shard_map/jit(dynamic_index_in_dim)/dynamic_slice | solution.py:86
  381.8 6.2 %copy.21 = f32[2304,512]{1,0:T(8,128)} copy(f32[2304,512]{0,1:T(8,128)} %bitcast.47) | data formatting | bytes 9437184 | tf_op jit(solution)/shard_map/reshape | solution.py:87
  388.0 3.3 fusion.20
  391.3 0.1 reshape.158
  391.5 0.1 reshape.160
  391.7 0.2 convert_reduce_fusion.1
  391.9 0.3 dynamic_update_slice.12
  392.2 23.3 %all-reduce = (f32[4096]{0:T(1024)S(1)}, f32[4096]{0:T(1024)S(1)}, f32[1024]{0:T(1024)S(1)}, f32[1024]{0:T(1024)S(1)}) all-reduce(f32[4096]{0:T(1024)S(1)} %dynamic_update_slice.12, f32[4096]{0:T(1024)S(1)} %dynamic_update_slice.13, ...), channel_id=1, replica_groups=mesh['seq_0'=8,'seq_1'=2,'img_0'=4,'img_1'=2,'fsdp'=2] {'seq_0'}, use_global_device_ids=true, to_apply=%region_7.8 | all-reduce | flops 10240 | bytes 81920 | tf_op jit(solution)/shard_map/psum | solution.py:66
  415.5 5.9 %all-reduce.4 = (f32[4096]{0:T(1024)S(1)}, f32[4096]{0:T(1024)S(1)}, f32[1024]{0:T(1024)S(1)}, f32[1024]{0:T(1024)S(1)}) all-reduce(f32[4096]{0:T(1024)S(1)} %get-tuple-element.8, f32[4096]{0:T(1024)S(1)} %get-tuple-element.9, ...), channel_id=1, replica_groups=mesh['seq_0'=8,'seq_1'=2,'img_0'=4,'img_1'=2,'fsdp'=2] {'seq_1'}, use_global_device_ids=true, to_apply=%region_8.9 | all-reduce | flops 10240 | bytes 81920 | tf_op jit(solution)/shard_map/psum | solution.py:66
  421.4 14.4 %all-reduce.1 = (f32[4096]{0:T(1024)S(1)}, f32[4096]{0:T(1024)S(1)}, f32[1024]{0:T(1024)S(1)}, f32[1024]{0:T(1024)S(1)}) all-reduce(f32[4096]{0:T(1024)S(1)} %get-tuple-element.24, f32[4096]{0:T(1024)S(1)} %get-tuple-element.25, ...), channel_id=1, replica_groups=mesh['seq_0'=8,'seq_1'=2,'img_0'=4,'img_1'=2,'fsdp'=2] {'img_0'}, use_global_device_ids=true, to_apply=%region_9.10 | all-reduce | flops 10240 | bytes 81920 | tf_op jit(solution)/shard_map/psum | solution.py:66
  435.7 10.3 %all-reduce.3 = (f32[4096]{0:T(1024)S(1)}, f32[4096]{0:T(1024)S(1)}, f32[1024]{0:T(1024)S(1)}, f32[1024]{0:T(1024)S(1)}) all-reduce(f32[4096]{0:T(1024)S(1)} %get-tuple-element.12, f32[4096]{0:T(1024)S(1)} %get-tuple-element.13, ...), channel_id=1, replica_groups=mesh['seq_0'=8,'seq_1'=2,'img_0'=4,'img_1'=2,'fsdp'=2] {'img_1'}, use_global_device_ids=true, to_apply=%region_10.11 | all-reduce | flops 10240 | bytes 81920 | tf_op jit(solution)/shard_map/psum | solution.py:66
  446.0 16.1 %all-reduce.2 = (f32[4096]{0:T(1024)}, f32[4096]{0:T(1024)}, f32[1024]{0:T(1024)}, f32[1024]{0:T(1024)}) all-reduce(f32[4096]{0:T(1024)S(1)} %get-tuple-element.20, f32[4096]{0:T(1024)S(1)} %get-tuple-element.21, f32[1024]{0:T(1024)S(1)} %get-tuple-element.22, ...), channel_id=1, replica_groups=mesh['seq_0'=8,'seq_1'=2,'img_0'=4,'img_1'=2,'fsdp'=2] {'fsdp'}, use_global_device_ids=true, to_apply=%region_11.12 | all-reduce | flops 10240 | bytes 81920 | tf_op jit(solution)/shard_map/psum | solution.py:66
  462.1 0.8 slice.12
  462.9 0.6 reshape.152
  463.6 1.0 slice.13
  464.6 0.7 reshape.153
  (58 shorter events, 0.6 us)
Async XLA Ops:
  7.2 315.1 %copy-start = (bf16[256,2048]{1,0:T(8,128)(2,1)S(1)}, bf16[256,2048]{1,0:T(8,128)(2,1)}, u32[]{:S(2)}) copy-start(bf16[256,2048]{1,0:T(8,128)(2,1)} %param.14) | copy-start | bytes 3145732
  7.2 44.5 %copy-start.13 = (s32[1,2]{1,0:T(1,128)S(1)}, s32[1,2]{1,0:T(1,128)}, u32[]{:S(2)}) copy-start(s32[1,2]{1,0:T(1,128)} %param.16) | copy-start | bytes 28
  7.2 44.8 %copy-start.9 = (s32[1,2304]{1,0:T(1,128)S(1)}, s32[1,2304]{1,0:T(1,128)}, u32[]{:S(2)}) copy-start(s32[1,2304]{1,0:T(1,128)} %param.17) | copy-start | bytes 27652
  7.2 44.4 %all-gather.9.cloned.1.call-start = ((), (), s32[]{:S(2)}) async-start(), calls=%async_computation.5 | async-start | bytes 3145728 | tf_op jit(solution)/shard_map/all_gather | solution.py:36
  7.9 114.2 %all-gather.7.cloned.1.call-start = ((), (), s32[]{:S(2)}) async-start(), calls=%async_computation.4 | async-start | bytes 4866048 | tf_op jit(solution)/shard_map/all_gather | solution.py:128
  8.7 287.3 %all-gather.11.cloned.1.call-start = ((), (), s32[]{:S(2)}) async-start(), calls=%async_computation.6 | async-start | bytes 18874368 | tf_op jit(solution)/shard_map/all_gather | solution.py:36
  128.9 3.8 copy-start.2
  132.6 1.3 copy-start.10
  132.6 1.3 copy-start.11
  138.7 2.1 copy-start.3
  327.8 9.2 %copy-start.8 = (bf16[512,256]{1,0:T(8,128)(2,1)S(1)}, bf16[512,256]{1,0:T(8,128)(2,1)}, u32[]{:S(2)}) copy-start(bf16[512,256]{1,0:T(8,128)(2,1)} %param.12) | copy-start | bytes 786436
  337.9 8.3 %all-to-all-start.1 = ((bf16[2,512,256]{2,1,0:T(8,128)(2,1)}), bf16[2,512,256]{2,1,0:T(8,128)(2,1)S(1)}, u32[]{:S(2)}, u32[]{:S(2)}) async-start(bf16[2,512,256]{2,1,0:T(8,128)(2,1)} %broadcast_in_dim.7), calls=%async_computation.1 | async-start | bytes 1048576 | tf_op jit(solution)/shard_map/all_to_all | solution.py:19
  341.7 4.5 copy-start.12
  341.7 120.4 %reduce-scatter.2.cloned.1.call-start = ((), (), s32[]{:S(2)}) async-start(), calls=%async_computation.3 | async-start | bytes 2949120 | tf_op jit(solution)/shard_map/reduce_scatter | solution.py:56
  341.7 11.2 %slice-start = ((s8[9437184]{0:T(1024)(128)(4,1)}), s8[1048576]{0:T(1024)(128)(4,1)S(1)}, s32[]{:S(2)}) async-start(s8[9437184]{0:T(1024)(128)(4,1)} %bitcast.44), calls=%async_computation.7 | async-start | bytes 2097152
  346.2 6.7 %copy-start.6 = (bf16[2,512,256]{2,1,0:T(8,128)(2,1)}, bf16[2,512,256]{2,1,0:T(8,128)(2,1)S(1)}, u32[]{:S(2)}) copy-start(bf16[2,512,256]{2,1,0:T(8,128)(2,1)S(1)} %all-to-all-done.1) | copy-start | bytes 1572868
  346.2 6.7 %slice-start.1 = ((s8[9437184]{0:T(1024)(128)(4,1)}), s8[4194304]{0:T(1024)(128)(4,1)S(1)}, s32[]{:S(2)}) async-start(s8[9437184]{0:T(1024)(128)(4,1)} %bitcast.44), calls=%async_computation.8 | async-start | bytes 8388608
  346.2 6.7 %slice-start.2 = ((s8[9437184]{0:T(1024)(128)(4,1)}), s8[4194304]{0:T(1024)(128)(4,1)S(1)}, s32[]{:S(2)}) async-start(s8[9437184]{0:T(1024)(128)(4,1)} %bitcast.44), calls=%async_computation.9 | async-start | bytes 8388608
  367.1 9.1 %copy-start.4 = (bf16[1,256,2048]{2,1,0:T(8,128)(2,1)S(1)}, bf16[1,256,2048]{2,1,0:T(8,128)(2,1)}, u32[]{:S(2)}) copy-start(bf16[1,256,2048]{2,1,0:T(8,128)(2,1)} %param.15) | copy-start | bytes 3145732
  367.1 9.6 %copy-start.7 = (bf16[2,512,256]{2,1,0:T(8,128)(2,1)S(1)}, bf16[2,512,256]{2,1,0:T(8,128)(2,1)}, u32[]{:S(2)}) copy-start(bf16[2,512,256]{2,1,0:T(8,128)(2,1)} %copy-done.6) | copy-start | bytes 1572868
  381.8 6.3 %copy-start.5 = (bf16[2304,256]{1,0:T(8,128)(2,1)S(1)}, bf16[2304,256]{1,0:T(8,128)(2,1)}, u32[]{:S(2)}) copy-start(bf16[2304,256]{1,0:T(8,128)(2,1)} %get-tuple-element.30) | copy-start | bytes 3538948
  388.0 77.3 %copy-start.1 = (bf16[256,2048]{1,0:T(8,128)(2,1)S(1)}, bf16[256,2048]{1,0:T(8,128)(2,1)}, u32[]{:S(2)}) copy-start(bf16[256,2048]{1,0:T(8,128)(2,1)} %param.14) | copy-start | bytes 3145732
Sparse Core Ops, SparseCore 0:
  9.8 41.7 all-gather.8
  53.5 68.5 all-gather.6
  123.9 172.0 all-gather.10
  367.2 79.7 reduce-scatter.1
where the time goes:
time: 473 us; the launch traced here: 472 us
  waiting for transfers between devices  268 us (57%)
  blocking collectives  79.1 us (17%)
  local copies, waits for them, and re-layouts  68.7 us (15%)
  matrix products  22.2 us (5%)
  other arithmetic  16 us (3%)
  between operations  14 us (3%)
    all_gather x2, waiting for transfers between devices, whole_of(): nearer = lax.all_gather(array, axes[-1], axis=dim, tiled=True)  196 us
    all_gather x1, waiting for transfers between devices, per_device(): gathered = lax.all_gather(vision_feats[0], SEQ_FSDP, axis=0, tiled=True)  70 us
    psum x5, blocking collectives, one_axis_at_a_time(): array = lax.psum(array, axis)  69.9 us
    gather x1, local copies, waits for them, and re-layouts, per_device(): picked = whole_grad[abs_pos]  26.2 us
    dot_general x4, matrix products, contract(): lax.dot_general(left, right, (((left_dim,), (right_dim,)), ((), ())), pre...  15.2 us
  transfers between devices with their start and end apart: 5, of which 3 were waited for; matrix products, arithmetic and copies ran while one was open for 10% of the time, Pallas kernels for 0%

commit v1 on v0

--- a/solution.py
+++ b/solution.py
@@ -63,7 +63,7 @@
 
 def one_axis_at_a_time(array, axes):
     for axis in axes:
-        array = lax.psum(array, axis)
+        array = jnp.sum(lax.all_gather(array, axis), axis=0)
     return array
 
 

time: 473 us -> 600 us (1.27)
  blocking collectives: 79.1 us -> 204 us
    all_gather x0 -> x20, blocking collectives: none -> 195 us  [one_axis_at_a_time(): array = jnp.sum(lax.all_gather(array, axis), axis=0)]
    psum x5 -> x0, blocking collectives: 69.9 us -> none  [one_axis_at_a_time(): array = lax.psum(array, axis)]
  transfers between devices with their start and end apart: 5 -> 5, of which waited for: 3 -> 3; matrix products, arithmetic and copies ran while one was open for 10% -> 8% of each run, Pallas kernels for 0% -> 0%
where the time goes in v1:
time: 600 us
  waiting for transfers between devices  268 us (45%)
  blocking collectives  204 us (34%)
  local copies, waits for them, and re-layouts  68.3 us (11%)
  matrix products  22.2 us (4%)
  other arithmetic  19.1 us (3%)
  between operations  14.1 us (2%)
    all_gather x2, waiting for transfers between devices, whole_of(): nearer = lax.all_gather(array, axes[-1], axis=dim, tiled=True)  196 us
    all_gather x20, blocking collectives, one_axis_at_a_time(): array = jnp.sum(lax.all_gather(array, axis), axis=0)  195 us
    all_gather x1, waiting for transfers between devices, per_device(): gathered = lax.all_gather(vision_feats[0], SEQ_FSDP, axis=0, tiled=True)  70 us
    gather x1, local copies, waits for them, and re-layouts, per_device(): picked = whole_grad[abs_pos]  26.2 us
    dot_general x4, matrix products, contract(): lax.dot_general(left, right, (((left_dim,), (right_dim,)), ((), ())), pre...  15.2 us
  transfers between devices with their start and end apart: 5, of which 3 were waited for; matrix products, arithmetic and copies ran while one was open for 8% of the time, Pallas kernels for 0%

profile of v1, /device:TPU:1, one launch (start us, length us, event | category | flops | bytes accessed | tf_op | source)
XLA Modules:
  0.0 599.6 jit_solution(4410289819049624668)
XLA Ops:
  8.7 42.9 %all-gather.29.cloned.1.call-done = bf16[1,512,2048]{2,1,0:T(8,128)(2,1)} async-done(((bf16[1,256,2048]{2,1,0:T(8,128)(2,1)}), bf16[1,512,2048]{2,1,0:T(8,128)(2,1)}) %all-gather.29.cloned.1.call-update) | async-done | bytes 2097168 | tf_op jit(solution)/shard_map/all_gather | solution.py:36
  52.0 70.0 %all-gather.27.cloned.1.call-done = bf16[1,2304,1024]{2,1,0:T(8,128)(2,1)} async-done(((bf16[1,72,1024]{2,1,0:T(8,128)(2,1)}), bf16[1,2304,1024]{2,1,0:T(8,128)(2,1)}) %all-gather.27.cloned.1.call-update) | async-done | bytes 4718608 | tf_op jit(solution)/shard_map/all_gather | solution.py:128
  122.1 6.8 %copy.20 = bf16[1,2304,1024]{1,2,0:T(8,128)(2,1)} copy(bf16[1,2304,1024]{2,1,0:T(8,128)(2,1)} %all-gather.27.cloned.1.call-done) | data formatting | bytes 9437184 | tf_op jit(solution)/shard_map/all_gather | solution.py:128
  128.9 3.2 convert_reduce_fusion
  132.6 1.3 fusion.3
  133.9 4.8 fusion.1
  138.7 2.1 copy-done.3
  140.9 1.6 constant_dynamic-slice_fusion.2
  142.5 153.5 %all-gather.31.cloned.1.call-done = bf16[1,4096,2048]{2,1,0:T(8,128)(2,1)} async-done(((bf16[1,512,2048]{2,1,0:T(8,128)(2,1)}), bf16[1,4096,2048]{2,1,0:T(8,128)(2,1)}) %all-gather.31.cloned.1.call-update) | async-done | bytes 16777232 | tf_op jit(solution)/shard_map/all_gather | solution.py:36
  296.0 26.2 %gather_fusion = bf16[2304,2048]{1,0:T(8,128)(2,1)} fusion(bf16[4096,2048]{1,0:T(8,128)(2,1)} %bitcast.49, s32[3072]{0:T(1024)S(1)} %pad_clamp_fusion), kind=kCustom, calls=%fused_computation | custom fusion | bytes 18883584 | tf_op jit(solution)/shard_map/gather | solution.py:140
  322.2 5.2 fusion.21
  327.8 9.2 %all_to_all.10 = f32[2,2304,256]{2,1,0:T(8,128)} all-to-all(f32[2,2304,256]{2,1,0:T(8,128)S(1)} %broadcast_in_dim.6), channel_id=1, replica_groups=mesh['seq_0'=8,'seq_1'=2,'img_0'=4,'img_1'=2,'fsdp'=2] {'fsdp'}, dimensions={0} | all-to-all | bytes 9437184 | tf_op jit(solution)/shard_map/all_to_all | solution.py:19
  337.0 0.8 broadcast_in_dim.7
  337.8 3.8 all-to-all-start.1
  341.7 4.5 reduce_sum.246
  346.2 6.7 %fusion.9 = (bf16[2304,256]{1,0:T(8,128)(2,1)}, f32[2304,256]{1,0:T(8,128)S(1)}) fusion(f32[2304,256]{1,0:T(8,128)} %reduce_sum.246, f32[256]{0:T(256)S(1)} %copy-done.12, bf16[2304,1024]{0,1:T(8,128)(2,1)} %copy-done.3, bf16[1024,256]{1,0:T(8,128)(2,1)S(1)} %bitcast.56), kind=kOutput, calls=%fused_computation.18 | convolution fusion | flops 1214447616 | bytes 11142144 | tf_op jit(solution)/shard_map/dot_general | solution.py:135
  352.9 4.0 fusion.11
  356.9 2.0 reshape_reshape.7
  358.9 2.8 fusion.22
  361.8 1.7 pad_maximum_fusion
  363.5 3.6 reshape.149
  367.1 9.0 %scatter_custom_fusion = f32[4096]{0:T(1024)S(1)} fusion(s32[2304]{0:T(1024)S(1)} %fusion.17, f32[2304]{0:T(1024)S(1)} %broadcast.83, f32[]{:T(128)} %constant.22.clone.1), kind=kCustom, calls=%fused_computation.40 | custom fusion | bytes 16388 | tf_op jit(solution)/shard_map/scatter | solution.py:116
  376.5 19.8 %all-gather.20 = f32[8,1,4096]{2,1,0:T(1,128)S(1)} all-gather(f32[1,1,4096]{2,1,0:T(1,128)S(1)} %fusion.10), channel_id=1, replica_groups=mesh['seq_0'=8,'seq_1'=2,'img_0'=4,'img_1'=2,'fsdp'=2] {'seq_0'}, dimensions={0}, use_global_device_ids=true | all-gather | bytes 147456 | tf_op jit(solution)/shard_map/all_gather | solution.py:66
  396.4 3.7 all-gather.7
  400.2 9.6 %all-gather.8 = f32[16384]{0:T(1024)S(1)} all-gather(f32[4096]{0:T(1024)S(1)} %reduce_sum.254), channel_id=10, replica_groups=mesh['seq_0'=8,'seq_1'=2,'img_0'=4,'img_1'=2,'fsdp'=2] {'img_0'}, dimensions={0}, use_global_device_ids=true | all-gather | bytes 81920 | tf_op jit(solution)/shard_map/all_gather | solution.py:66
  409.8 4.8 all-gather.9
  414.7 11.0 %all-gather.10 = f32[8192]{0:T(1024)S(1)} all-gather(f32[4096]{0:T(1024)S(1)} %reduce_sum.256), channel_id=12, replica_groups=mesh['seq_0'=8,'seq_1'=2,'img_0'=4,'img_1'=2,'fsdp'=2] {'fsdp'}, dimensions={0}, use_global_device_ids=true | all-gather | bytes 49152 | tf_op jit(solution)/shard_map/all_gather | solution.py:66
  426.3 4.8 constant_dynamic-slice_fusion
  431.2 6.3 %copy.21 = f32[2304,512]{1,0:T(8,128)} copy(f32[2304,512]{0,1:T(8,128)} %bitcast.53) | data formatting | bytes 9437184 | tf_op jit(solution)/shard_map/reshape | solution.py:87
  437.7 19.4 %all-gather.19 = f32[8,1,4096]{2,1,0:T(1,128)S(1)} all-gather(f32[1,1,4096]{2,1,0:T(1,128)S(1)} %constant_dynamic-update-slice_fusion), channel_id=1, replica_groups=mesh['seq_0'=8,'seq_1'=2,'img_0'=4,'img_1'=2,'fsdp'=2] {'seq_0'}, dimensions={0}, use_global_device_ids=true | all-gather | bytes 147456 | tf_op jit(solution)/shard_map/all_gather | solution.py:66
  457.2 3.3 all-gather.3
  460.5 9.0 %all-gather.4 = f32[16384]{0:T(1024)S(1)} all-gather(f32[4096]{0:T(1024)S(1)} %reduce_sum.249), channel_id=6, replica_groups=mesh['seq_0'=8,'seq_1'=2,'img_0'=4,'img_1'=2,'fsdp'=2] {'img_0'}, dimensions={0}, use_global_device_ids=true | all-gather | bytes 81920 | tf_op jit(solution)/shard_map/all_gather | solution.py:66
  469.5 4.8 all-gather.5
  474.4 12.1 %all-gather.6 = f32[8192]{0:T(1024)S(1)} all-gather(f32[4096]{0:T(1024)S(1)} %reduce_sum.251), channel_id=8, replica_groups=mesh['seq_0'=8,'seq_1'=2,'img_0'=4,'img_1'=2,'fsdp'=2] {'fsdp'}, dimensions={0}, use_global_device_ids=true | all-gather | bytes 49152 | tf_op jit(solution)/shard_map/all_gather | solution.py:66
  486.6 3.2 fusion.20
  490.0 18.3 %all-gather.21 = f32[8,1,1024]{2,1,0:T(1,128)S(1)} all-gather(f32[1,1,1024]{2,1,0:T(1,128)S(1)} %reshape.198), channel_id=1, replica_groups=mesh['seq_0'=8,'seq_1'=2,'img_0'=4,'img_1'=2,'fsdp'=2] {'seq_0'}, dimensions={0}, use_global_device_ids=true | all-gather | bytes 36864 | tf_op jit(solution)/shard_map/all_gather | solution.py:66
  508.3 3.2 all-gather.11
  511.6 9.1 %all-gather.12 = f32[4096]{0:T(1024)S(1)} all-gather(f32[1024]{0:T(1024)S(1)} %reduce_sum.260), channel_id=14, replica_groups=mesh['seq_0'=8,'seq_1'=2,'img_0'=4,'img_1'=2,'fsdp'=2] {'img_0'}, dimensions={0}, use_global_device_ids=true | all-gather | bytes 20480 | tf_op jit(solution)/shard_map/all_gather | solution.py:66
  520.7 4.7 all-gather.13
  525.5 13.4 %all-gather.14 = f32[2048]{0:T(1024)S(1)} all-gather(f32[1024]{0:T(1024)S(1)} %reduce_sum.262), channel_id=16, replica_groups=mesh['seq_0'=8,'seq_1'=2,'img_0'=4,'img_1'=2,'fsdp'=2] {'fsdp'}, dimensions={0}, use_global_device_ids=true | all-gather | bytes 12288 | tf_op jit(solution)/shard_map/all_gather | solution.py:66
  539.1 18.3 %all-gather.22 = f32[8,1,1024]{2,1,0:T(1,128)S(1)} all-gather(f32[1,1,1024]{2,1,0:T(1,128)S(1)} %reshape.200), channel_id=1, replica_groups=mesh['seq_0'=8,'seq_1'=2,'img_0'=4,'img_1'=2,'fsdp'=2] {'seq_0'}, dimensions={0}, use_global_device_ids=true | all-gather | bytes 36864 | tf_op jit(solution)/shard_map/all_gather | solution.py:66
  557.4 3.2 all-gather.15
  560.7 9.1 %all-gather.16 = f32[4096]{0:T(1024)S(1)} all-gather(f32[1024]{0:T(1024)S(1)} %reduce_sum.266), channel_id=18, replica_groups=mesh['seq_0'=8,'seq_1'=2,'img_0'=4,'img_1'=2,'fsdp'=2] {'img_0'}, dimensions={0}, use_global_device_ids=true | all-gather | bytes 20480 | tf_op jit(solution)/shard_map/all_gather | solution.py:66
  569.8 4.7 all-gather.17
  574.6 13.4 %all-gather.18 = f32[2048]{0:T(1024)S(1)} all-gather(f32[1024]{0:T(1024)S(1)} %reduce_sum.268), channel_id=20, replica_groups=mesh['seq_0'=8,'seq_1'=2,'img_0'=4,'img_1'=2,'fsdp'=2] {'fsdp'}, dimensions={0}, use_global_device_ids=true | all-gather | bytes 12288 | tf_op jit(solution)/shard_map/all_gather | solution.py:66
  589.8 0.8 slice.12
  591.3 1.0 slice.13
  592.3 0.7 reshape.151
  (108 shorter events, 7.9 us)
Async XLA Ops:
  7.2 315.1 %copy-start = (bf16[256,2048]{1,0:T(8,128)(2,1)S(1)}, bf16[256,2048]{1,0:T(8,128)(2,1)}, u32[]{:S(2)}) copy-start(bf16[256,2048]{1,0:T(8,128)(2,1)} %param.14) | copy-start | bytes 3145732
  7.2 44.5 %copy-start.13 = (s32[1,2]{1,0:T(1,128)S(1)}, s32[1,2]{1,0:T(1,128)}, u32[]{:S(2)}) copy-start(s32[1,2]{1,0:T(1,128)} %param.16) | copy-start | bytes 28
  7.2 44.8 %copy-start.9 = (s32[1,2304]{1,0:T(1,128)S(1)}, s32[1,2304]{1,0:T(1,128)}, u32[]{:S(2)}) copy-start(s32[1,2304]{1,0:T(1,128)} %param.17) | copy-start | bytes 27652
  7.2 44.4 %all-gather.29.cloned.1.call-start = ((), (), s32[]{:S(2)}) async-start(), calls=%async_computation.5 | async-start | bytes 3145728 | tf_op jit(solution)/shard_map/all_gather | solution.py:36
  7.9 114.2 %all-gather.27.cloned.1.call-start = ((), (), s32[]{:S(2)}) async-start(), calls=%async_computation.4 | async-start | bytes 4866048 | tf_op jit(solution)/shard_map/all_gather | solution.py:128
  8.7 287.3 %all-gather.31.cloned.1.call-start = ((), (), s32[]{:S(2)}) async-start(), calls=%async_computation.6 | async-start | bytes 18874368 | tf_op jit(solution)/shard_map/all_gather | solution.py:36
  128.9 3.8 copy-start.2
  132.6 1.3 copy-start.10
  132.6 1.3 copy-start.11
  138.7 2.1 copy-start.3
  327.8 9.2 %copy-start.8 = (bf16[512,256]{1,0:T(8,128)(2,1)S(1)}, bf16[512,256]{1,0:T(8,128)(2,1)}, u32[]{:S(2)}) copy-start(bf16[512,256]{1,0:T(8,128)(2,1)} %param.12) | copy-start | bytes 786436
  337.8 8.3 %all-to-all-start.1 = ((bf16[2,512,256]{2,1,0:T(8,128)(2,1)}), bf16[2,512,256]{2,1,0:T(8,128)(2,1)S(1)}, u32[]{:S(2)}, u32[]{:S(2)}) async-start(bf16[2,512,256]{2,1,0:T(8,128)(2,1)} %broadcast_in_dim.7), calls=%async_computation.1 | async-start | bytes 1048576 | tf_op jit(solution)/shard_map/all_to_all | solution.py:19
  341.7 4.5 copy-start.12
  341.7 248.1 %reduce-scatter.2.cloned.1.call-start = ((), (), s32[]{:S(2)}) async-start(), calls=%async_computation.3 | async-start | bytes 2949120 | tf_op jit(solution)/shard_map/reduce_scatter | solution.py:56
  341.7 11.2 %slice-start = ((s8[9437184]{0:T(1024)(128)(4,1)}), s8[1048576]{0:T(1024)(128)(4,1)S(1)}, s32[]{:S(2)}) async-start(s8[9437184]{0:T(1024)(128)(4,1)} %bitcast.50), calls=%async_computation.7 | async-start | bytes 2097152
  346.2 6.7 %copy-start.6 = (bf16[2,512,256]{2,1,0:T(8,128)(2,1)}, bf16[2,512,256]{2,1,0:T(8,128)(2,1)S(1)}, u32[]{:S(2)}) copy-start(bf16[2,512,256]{2,1,0:T(8,128)(2,1)S(1)} %all-to-all-done.1) | copy-start | bytes 1572868
  346.2 6.7 %slice-start.1 = ((s8[9437184]{0:T(1024)(128)(4,1)}), s8[4194304]{0:T(1024)(128)(4,1)S(1)}, s32[]{:S(2)}) async-start(s8[9437184]{0:T(1024)(128)(4,1)} %bitcast.50), calls=%async_computation.8 | async-start | bytes 8388608
  346.2 6.7 %slice-start.2 = ((s8[9437184]{0:T(1024)(128)(4,1)}), s8[4194304]{0:T(1024)(128)(4,1)S(1)}, s32[]{:S(2)}) async-start(s8[9437184]{0:T(1024)(128)(4,1)} %bitcast.50), calls=%async_computation.9 | async-start | bytes 8388608
  367.1 9.2 %copy-start.4 = (bf16[1,256,2048]{2,1,0:T(8,128)(2,1)S(1)}, bf16[1,256,2048]{2,1,0:T(8,128)(2,1)}, u32[]{:S(2)}) copy-start(bf16[1,256,2048]{2,1,0:T(8,128)(2,1)} %param.15) | copy-start | bytes 3145732
  367.1 59.2 %copy-start.7 = (bf16[2,512,256]{2,1,0:T(8,128)(2,1)S(1)}, bf16[2,512,256]{2,1,0:T(8,128)(2,1)}, u32[]{:S(2)}) copy-start(bf16[2,512,256]{2,1,0:T(8,128)(2,1)} %copy-done.6) | copy-start | bytes 1572868
  431.2 6.3 %copy-start.5 = (bf16[2304,256]{1,0:T(8,128)(2,1)S(1)}, bf16[2304,256]{1,0:T(8,128)(2,1)}, u32[]{:S(2)}) copy-start(bf16[2304,256]{1,0:T(8,128)(2,1)} %get-tuple-element.10) | copy-start | bytes 3538948
  486.5 106.5 %copy-start.1 = (bf16[256,2048]{1,0:T(8,128)(2,1)S(1)}, bf16[256,2048]{1,0:T(8,128)(2,1)}, u32[]{:S(2)}) copy-start(bf16[256,2048]{1,0:T(8,128)(2,1)} %param.14) | copy-start | bytes 3145732
Sparse Core Ops, SparseCore 0:
  9.8 41.7 all-gather.28
  53.5 68.5 all-gather.26
  123.9 172.0 all-gather.30
  367.2 79.6 reduce-scatter.1
